TPU v7x, 32 devices: a whole 2x2x4 slice. The times are simulated.
32 devices in a mesh: gx: 8 (over z, x), gy: 4 (over y, core).
Axes of the slice: x: 2, y: 2, z: 4, core: 2. Of those that a mesh axis runs over, the one named last changes fastest.
Arguments:
- start_field: bfloat16 [6, 1280, 1024], P(None, 'gx', 'gy'), may hold values from -6 to 6
- tensor: bfloat16 [6, 1280, 1024], P(None, 'gx', 'gy'), may hold values from -6 to 20, as said below
- class_map: int32 [80, 64], P('gx', 'gy'), may hold values from 0 to 1, as said below
Outputs:
- mode_field: float32 [6, 1280, 1024], P(None, 'gx', 'gy')
- estimate: float32 [], replicated
Inputs may be any that keep to these rules, and one draw needn't show every extreme that they name: `tensor`: entries 0 to 2 of a cell are positive, entries 3 to 5 are its off-diagonal entries. `class_map`: 1 marks a tile whose cells use the full tensor, 0 a tile that uses its diagonal only.
All inputs are finite; a program needn't handle non-finite values.
Results may differ from a plain program's by a relative error of at most 0.00035.
Values may be sent and summed in bfloat16 or wider, within the bound.
No kernel may reach another device: no remote copies, remote signals or barrier semaphores. Data moves between devices by JAX's collectives and lax.ppermute only.
A program may use at most 64 MiB of HBM per device.

v0:
```python
import jax
import jax.numpy as jnp
from jax import lax
from jax.experimental import pallas as pl
from jax.experimental.pallas import tpu as pltpu
from jax.sharding import PartitionSpec as P

TILE = 16
ITERS = 4
LANES = 128
SUB = 8
STRIP = 16
LOW = 13
HIGH = 14
PAD = 24
epsilon = 1e-06
f32 = jnp.float32
bf16 = jnp.bfloat16
FIELD_SCALE = (18.0, 18.0, 1.0, 18.0, 18.0, 1.0)
TENSOR_SCALE = (
    1.0 / 576.0,
    1.0 / 576.0,
    1.0 / (576.0 * 324.0),
    1.0 / 576.0,
    1.0 / (576.0 * 18.0),
    1.0 / (576.0 * 18.0),
)
BELOW = 324.0


def lane_index(rows):
    return lax.broadcasted_iota(jnp.int32, (rows, LANES), 1)


def shifted(value, amount):
    amount = amount % LANES
    return value if amount == 0 else pltpu.roll(value, amount, 1)


def heavy_cells(class_map, rows, cols):
    tiles_x, tiles_y = class_map.shape
    row_of = lax.broadcasted_iota(jnp.int32, (rows, tiles_x), 0) // TILE
    row_pick = (row_of == lax.broadcasted_iota(jnp.int32, (rows, tiles_x), 1)).astype(f32)
    col_of = lax.broadcasted_iota(jnp.int32, (tiles_y, cols), 1) // TILE
    col_pick = (col_of == lax.broadcasted_iota(jnp.int32, (tiles_y, cols), 0)).astype(f32)
    spread = jnp.dot(row_pick, class_map.astype(f32), preferred_element_type=f32)
    return jnp.dot(spread, col_pick, preferred_element_type=f32)


def pack_kernel(start, tensor, class_map, left, right, top, bottom, mask):
    rows, cols = start.shape[1:]
    mask[...] = heavy_cells(class_map[...], rows, cols)

    def source(index, first):
        if index < 6:
            return start[index, pl.ds(first, STRIP), :].astype(f32)
        value = tensor[index - 6, pl.ds(first, STRIP), :].astype(f32)
        if index >= 9:
            value = value * mask[pl.ds(first, STRIP), :]
        return value

    lanes = lane_index(STRIP)
    last = cols - LANES
    per = LANES // STRIP

    def block(step, carry):
        first = pl.multiple_of(step * STRIP, STRIP)
        for group in range(2):
            low_part = jnp.zeros((STRIP, LANES), f32)
            high_part = jnp.zeros((STRIP, LANES), f32)
            for index in range(group * per, min(12, (group + 1) * per)):
                value = source(index, first)
                place = STRIP * (index % per)
                here = (lanes >= place) & (lanes < place + STRIP)
                low_part = jnp.where(here, shifted(value[:, :LANES], place), low_part)
                high_part = jnp.where(here, shifted(value[:, last:], place + STRIP), high_part)
            left[pl.ds(first, STRIP), group * LANES : (group + 1) * LANES] = low_part.astype(bf16)
            right[pl.ds(first, STRIP), group * LANES : (group + 1) * LANES] = high_part.astype(bf16)
        return carry

    lax.fori_loop(0, rows // STRIP, block, 0)
    for index in range(12):
        top[index * STRIP : (index + 1) * STRIP, :] = source(index, 0).astype(bf16)
        bottom[index * STRIP : (index + 1) * STRIP, :] = source(index, rows - STRIP).astype(bf16)


def forward(centre, plus, plus2, minus):
    return 27.0 * (plus - centre) - (plus2 - minus)


def main_kernel(
    row_parts, width, start, tensor, class_map, left, right, above, below, out, sums, field, flux, coef, mask, keep, keep2, inner
):
    rows, cols = start.shape[1:]
    tiles = field.shape[0]
    per = LANES // STRIP
    row_base = lax.axis_index("gx") * rows
    col_base = lax.axis_index("gy") * cols
    total_rows = rows * lax.axis_size("gx")
    total_cols = cols * lax.axis_size("gy")
    mask[...] = heavy_cells(class_map[...], rows, cols)
    deep = field.shape[2]

    for tile in range(tiles):
        r = lax.broadcasted_iota(jnp.int32, (deep, LANES), 0) - PAD
        c = lax.broadcasted_iota(jnp.int32, (deep, LANES), 1) + (tile * width - LOW)
        gr, gc = r + row_base, c + col_base
        good = (gr >= 0) & (gr < total_rows) & (gc >= 0) & (gc < total_cols)
        keep[tile] = jnp.where(good, 1.0, 0.0)
        keep2[tile] = jnp.where(good, BELOW, 0.0)
        lo = tile * width
        mine = (r >= 0) & (r < rows) & (c >= lo) & (c < min(cols, lo + width))
        inner[tile] = jnp.where(mine, 1.0, 0.0)
        edge = jnp.zeros((SUB, LANES), f32)
        for index in range(6):
            for first in (0, deep - SUB):
                field[tile, index, first : first + SUB, :] = edge
                flux[tile, index, first : first + SUB, :] = edge

    lanes = lane_index(STRIP)

    def place(target, index, first, value, low_strip, high_strip, factor):
        value = value * factor
        spot = STRIP * (index % per)
        group = index // per
        low_part = low_strip[:, group * LANES : (group + 1) * LANES] * factor
        high_part = high_strip[:, group * LANES : (group + 1) * LANES] * factor
        which = index if index < 6 else index - 6
        for tile in range(tiles):
            base = tile * width - LOW
            result = jnp.zeros((STRIP, LANES), f32)
            if base < 0:
                result = jnp.where(lanes < -base, shifted(low_part, -(spot + STRIP + base)), result)
            for piece in range(cols // LANES):
                begin = piece * LANES - base
                if begin >= LANES or begin + LANES <= 0:
                    continue
                here = (lanes >= begin) & (lanes < begin + LANES)
                moved = shifted(value[:, piece * LANES : (piece + 1) * LANES], begin)
                result = jnp.where(here, moved, result)
            begin = cols - base
            if begin < LANES:
                here = (lanes >= begin) & (lanes < begin + STRIP)
                result = jnp.where(here, shifted(high_part, begin - spot), result)
            target[tile, which, pl.ds(first, STRIP), :] = result

    def assemble(step, carry):
        first = pl.multiple_of(step * STRIP, STRIP)
        low_strip = left[pl.ds(first, STRIP), :].astype(f32)
        high_strip = right[pl.ds(first, STRIP), :].astype(f32)
        for index in range(12):
            if index < 6:
                value = start[index, pl.ds(first, STRIP), :].astype(f32)
                place(field, index, PAD + first, value, low_strip, high_strip, FIELD_SCALE[index])
            else:
                value = tensor[index - 6, pl.ds(first, STRIP), :].astype(f32)
                if index >= 9:
                    value = value * mask[pl.ds(first, STRIP), :]
                place(coef, index, PAD + first, value, low_strip, high_strip, TENSOR_SCALE[index - 6])
        return carry

    lax.fori_loop(0, rows // STRIP, assemble, 0)
    for strip, first in ((above, PAD - STRIP), (below, PAD + rows)):
        low_strip = strip[12 * STRIP : 13 * STRIP, :].astype(f32)
        high_strip = strip[13 * STRIP : 14 * STRIP, :].astype(f32)
        for index in range(12):
            value = strip[index * STRIP : (index + 1) * STRIP, :].astype(f32)
            factor = FIELD_SCALE[index] if index < 6 else TENSOR_SCALE[index - 6]
            place(field if index < 6 else coef, index, first, value, low_strip, high_strip, factor)

    def load(ref, tile, index, first, offset):
        return ref[tile, index, pl.ds(first + offset, SUB), :]

    def curl_forward(ref, tile, first):
        out_parts = []
        centre = [load(ref, tile, index, first, 0) for index in range(6)]
        for part in range(2):
            sign = 1.0 if part == 0 else -1.0
            x, y, z = centre[3 * part : 3 * part + 3]
            ox, oy = centre[3 - 3 * part], centre[4 - 3 * part]
            zi, yi = 3 * part + 2, 3 * part + 1
            dyz = forward(z, shifted(z, -1), shifted(z, -2), shifted(z, 1))
            dxz = forward(
                z, load(ref, tile, zi, first, 1), load(ref, tile, zi, first, 2), load(ref, tile, zi, first, -1)
            )
            near = (load(ref, tile, yi, first, 1) - y) - (shifted(x, -1) - x)
            far = (load(ref, tile, yi, first, 2) - load(ref, tile, yi, first, -1)) - (shifted(x, -2) - shifted(x, 1))
            if part == 0:
                out_parts.append((dyz + oy, -(ox + dxz), 27.0 * near - far))
            else:
                out_parts.append((dyz - oy, ox - dxz, 27.0 * near - far))
        return out_parts

    def curl_backward(ref, tile, first):
        out_parts = []
        centre = [load(ref, tile, index, first, 0) for index in range(6)]
        for part in range(2):
            x, y, z = centre[3 * part : 3 * part + 3]
            ox, oy = centre[3 - 3 * part], centre[4 - 3 * part]
            zi, yi = 3 * part + 2, 3 * part + 1
            dyz = forward(shifted(z, 1), z, shifted(z, -1), shifted(z, 2))
            dxz = forward(
                load(ref, tile, zi, first, -1), z, load(ref, tile, zi, first, 1), load(ref, tile, zi, first, -2)
            )
            near = (y - load(ref, tile, yi, first, -1)) - (x - shifted(x, 1))
            far = (load(ref, tile, yi, first, 1) - load(ref, tile, yi, first, -2)) - (shifted(x, -1) - shifted(x, 2))
            if part == 0:
                out_parts.append((dyz + oy, -(ox + dxz), 27.0 * near - far))
            else:
                out_parts.append((dyz - oy, ox - dxz, 27.0 * near - far))
        return out_parts

    def contract(tile, first, parts):
        k = [load(coef, tile, index, first, 0) for index in range(6)]
        results = []
        for cx, cy, cz in parts:
            results.append(
                (
                    k[0] * cx + k[3] * cy + k[4] * cz,
                    k[3] * cx + k[1] * cy + k[5] * cz,
                    k[4] * cx + k[5] * cy + k[2] * cz,
                )
            )
        return results

    unroll = 4

    def over(span, body, carry):
        lo = (PAD + span[0]) // SUB * SUB
        hi = -(-(PAD + span[1]) // SUB) * SUB
        count = (hi - lo) // SUB

        def chunk(size, at, carry):
            for inside in range(size):
                carry = body(at + inside * SUB, carry)
            return carry

        whole = count // unroll

        def loop(step, carry):
            return chunk(unroll, pl.multiple_of(lo + step * (unroll * SUB), SUB), carry)

        carry = lax.fori_loop(0, whole, loop, carry)
        if count % unroll:
            carry = chunk(count % unroll, lo + whole * unroll * SUB, carry)
        return carry

    zero = jnp.zeros((SUB, LANES), f32)

    def run_tile(tile, totals):
        totals = list(totals)
        for turn in range(ITERS):
            reach = 3 * (ITERS - 1 - turn)

            def first_half(first, carry):
                m, m2 = keep[tile, pl.ds(first, SUB), :], keep2[tile, pl.ds(first, SUB), :]
                for part, (hx, hy, hz) in enumerate(curl_forward(field, tile, first)):
                    flux[tile, 3 * part, pl.ds(first, SUB), :] = hx * m2
                    flux[tile, 3 * part + 1, pl.ds(first, SUB), :] = hy * m2
                    flux[tile, 3 * part + 2, pl.ds(first, SUB), :] = hz * m
                return carry

            over((-3 - reach, rows + 3 + reach), first_half, 0)

            def second_half(first, carry):
                flat, upright = carry
                results = contract(tile, first, curl_backward(flux, tile, first))
                for part, triple in enumerate(results):
                    for axis in range(3):
                        field[tile, 3 * part + axis, pl.ds(first, SUB), :] = triple[axis]
                (ax, ay, az), (bx, by, bz) = results
                own = inner[tile, pl.ds(first, SUB), :]
                flat = flat + own * ((ax * ax + ay * ay) + (bx * bx + by * by))
                upright = upright + own * (az * az + bz * bz)
                return flat, upright

            flat, upright = over((-1 - reach, rows + 2 + reach), second_half, (zero, zero))
            totals[turn] = totals[turn] + (flat * (1.0 / 324.0) + upright)

        def weigh(first, carry):
            e = [load(field, tile, index, first, 0) for index in range(6)]
            parts = contract(tile, first, ((e[0], e[1], BELOW * e[2]), (e[3], e[4], BELOW * e[5])))
            for part, triple in enumerate(parts):
                for axis in range(3):
                    flux[tile, 3 * part + axis, pl.ds(first, SUB), :] = triple[axis]
            return carry

        over((-1, rows + 2), weigh, 0)

        def pair(first, carry):
            flat, upright = carry
            one = curl_forward(field, tile, first)
            two = curl_forward(flux, tile, first)
            own = inner[tile, pl.ds(first, SUB), :]
            flat = flat + own * (
                (one[0][0] * two[0][0] + one[0][1] * two[0][1]) + (one[1][0] * two[1][0] + one[1][1] * two[1][1])
            )
            upright = upright + own * (one[0][2] * two[0][2] + one[1][2] * two[1][2])
            return flat, upright

        flat, upright = over((0, rows), pair, (zero, zero))
        totals[ITERS] = totals[ITERS] + (flat + upright * (1.0 / 324.0))
        return tuple(totals)

    totals = lax.fori_loop(0, tiles, run_tile, (zero,) * (ITERS + 1))

    line_lanes = lax.broadcasted_iota(jnp.int32, (1, LANES), 1)
    line = jnp.zeros((1, LANES), f32)
    for number, total in enumerate(totals):
        amount = jnp.sum(jnp.sum(total, axis=0, keepdims=True), axis=1, keepdims=True)
        line = jnp.where(line_lanes == number, amount, line)
    sums[...] = jnp.broadcast_to(line, sums.shape)

    sub_lanes = lane_index(SUB)

    def collect(step, carry):
        first = pl.multiple_of(step * SUB, SUB)
        for index in range(6):
            for piece in range(cols // LANES):
                result = zero
                for tile in range(tiles):
                    begin = tile * width - piece * LANES
                    end = min(cols, (tile + 1) * width) - piece * LANES
                    if end <= 0 or begin >= LANES:
                        continue
                    moved = shifted(field[tile, index, pl.ds(PAD + first, SUB), :], begin - LOW)
                    here = (sub_lanes >= begin) & (sub_lanes < end)
                    result = jnp.where(here, moved, result)
                out[index, pl.ds(first, SUB), piece * LANES : (piece + 1) * LANES] = result
        return carry

    lax.fori_loop(0, rows // SUB, collect, 0)


def scale_kernel(cell_count, field, sums, out, estimate):
    totals = jnp.sum(sums[...], axis=0, keepdims=True)
    picks = [totals[:, number : number + 1] for number in range(ITERS + 1)]
    factor = jnp.ones((1, 1), f32)
    for number in range(ITERS):
        square_sum = factor * factor * picks[number]
        factor = factor * lax.rsqrt(square_sum / cell_count + epsilon)
    estimate[...] = picks[ITERS] / picks[ITERS - 1]
    flat = factor * (1.0 / 18.0)
    for index in range(6):
        out[index] = field[index] * (factor if index % 3 == 2 else flat)


def on_device(start_field, tensor, class_map):
    rows, cols = start_field.shape[1:]
    devices = lax.axis_size("gx") * lax.axis_size("gy")
    cell_count = rows * cols * devices
    tiles = -(-cols // (LANES - LOW - HIGH))
    width = -(-cols // tiles)
    whole = pl.BlockSpec(memory_space=pltpu.VMEM)
    strip_rows = 12 * STRIP
    left, right, top, bottom = pl.pallas_call(
        pack_kernel,
        out_shape=(
            jax.ShapeDtypeStruct((rows, 2 * LANES), bf16),
            jax.ShapeDtypeStruct((rows, 2 * LANES), bf16),
            jax.ShapeDtypeStruct((strip_rows, cols), bf16),
            jax.ShapeDtypeStruct((strip_rows, cols), bf16),
        ),
        in_specs=[whole] * 3,
        out_specs=(whole,) * 4,
        scratch_shapes=[pltpu.VMEM((rows, cols), f32)],
        name="pack",
    )(start_field, tensor, class_map)

    def both(low_going, high_going, axis):
        count = lax.axis_size(axis)
        up = [(i, i + 1) for i in range(count - 1)]
        down = [(j, i) for i, j in up]
        return lax.ppermute(high_going, axis, up), lax.ppermute(low_going, axis, down)

    from_left, from_right = both(left, right, "gy")
    top = jnp.concatenate([top, from_left[:STRIP], from_right[:STRIP]])
    bottom = jnp.concatenate([bottom, from_left[-STRIP:], from_right[-STRIP:]])
    above, below = both(top, bottom, "gx")
    deep = rows + 2 * PAD
    plane = pltpu.VMEM((tiles, deep, LANES), f32)
    stack = pltpu.VMEM((tiles, 6, deep, LANES), f32)

    def main(*refs):
        main_kernel(None, width, *refs)

    image, sums = pl.pallas_call(
        main,
        out_shape=(
            jax.ShapeDtypeStruct((6, rows, cols), f32),
            jax.ShapeDtypeStruct((devices, LANES), f32),
        ),
        in_specs=[whole] * 7,
        out_specs=(whole,) * 2,
        scratch_shapes=[stack, stack, stack, pltpu.VMEM((rows, cols), f32), plane, plane, plane],
        name="products",
    )(start_field, tensor, class_map, from_left, from_right, above, below)
    sums = lax.all_to_all(sums, ("gx", "gy"), 0, 0, tiled=True)

    def scale(*refs):
        scale_kernel(float(cell_count), *refs)

    mode, estimate = pl.pallas_call(
        scale,
        out_shape=(
            jax.ShapeDtypeStruct((6, rows, cols), f32),
            jax.ShapeDtypeStruct((1, 1), f32),
        ),
        in_specs=[whole] * 2,
        out_specs=(whole,) * 2,
        name="scale",
    )(image, sums)
    return mode, estimate[0, 0]


def solution(mesh):
    placed = (P(None, "gx", "gy"), P(None, "gx", "gy"), P("gx", "gy"))
    return jax.shard_map(
        on_device, mesh=mesh, in_specs=placed, out_specs=(P(None, "gx", "gy"), P()), check_vma=False
    )
```

profile of v0, /device:TPU:0, one launch (start us, length us, event | category | flops | bytes accessed | tf_op | source)
XLA Modules:
  0.0 67.7 jit_solution(5615683148003245799)
XLA Ops:
  0.6 3.1 %pack.1 = (bf16[160,256]{1,0:T(8,128)(2,1)}, bf16[160,256]{1,0:T(8,128)(2,1)}, bf16[192,256]{1,0:T(8,128)(2,1)}, bf16[192,256]{1,0:T(8,128)(2,1)}) custom-call(bf16[6,160,256]{2,1,0:T(8,128)(2,1)} %refs_0_.1, bf16[6,160,256]{2,1,0:T(8,128)(2,1)} %refs_1_.1, s32[10,16]{1,0:T(8,128)} %refs_2_.1), custom_call_target="tpu_custom_call" | custom-call | tf_op jit(solution)/shard_map/pack/pallas_call | solution.py:356
  3.8 2.4 %collective-permute-start = (bf16[160,256]{1,0:T(8,128)(2,1)}, bf16[160,256]{1,0:T(8,128)(2,1)S(1)}, u32[]{:S(2)}, u32[]{:S(2)}) collective-permute-start(bf16[160,256]{1,0:T(8,128)(2,1)} %get-tuple-element.10), channel_id=1, source_target_pairs={{0,1},{1,2},{2,3},{4,5},{5,6},{6,7},{8,9},{9,10},{10,11},{12,13},{... | collective-permute-start | bytes 245768 | tf_op jit(solution)/shard_map/ppermute | solution.py:374
  6.2 1.3 %collective-permute-start.1 = (bf16[160,256]{1,0:T(8,128)(2,1)}, bf16[160,256]{1,0:T(8,128)(2,1)S(1)}, u32[]{:S(2)}, u32[]{:S(2)}) collective-permute-start(bf16[160,256]{1,0:T(8,128)(2,1)} %get-tuple-element.11), channel_id=1, source_target_pairs={{1,0},{2,1},{3,2},{5,4},{6,5},{7,6},{9,8},{10,9},{11,10},{13,12},{... | collective-permute-start | bytes 245768 | tf_op jit(solution)/shard_map/ppermute | solution.py:374
  7.5 0.0 collective-permute-done.refs_3_
  7.5 0.0 copy-start
  7.5 4.2 %collective-permute-done.1.refs_4_ = bf16[160,256]{1,0:T(8,128)(2,1)S(1)} collective-permute-done((bf16[160,256]{1,0:T(8,128)(2,1)}, bf16[160,256]{1,0:T(8,128)(2,1)S(1)}, u32[]{:S(2)}, u32[]{:S(2)}) %collective-permute-start.1) | collective-permute-done | bytes 81952 | tf_op jit(solution)/shard_map/ppermute | solution.py:374
  11.7 0.0 copy-start.1
  11.7 0.0 copy-start.4
  11.7 0.9 %pad_maximum_fusion = bf16[224,256]{1,0:T(8,128)(2,1)S(1)} fusion(bf16[16,256]{1,0:T(8,128)(2,1)S(1)} %get-tuple-element.21, bf16[16,256]{1,0:T(8,128)(2,1)S(1)} %get-tuple-element.19, bf16[192,256]{1,0:T(8,128)(2,1)} %get-tuple-element.12), kind=kLoop, calls=%fused_computation | loop fusion | flops 344064 | bytes 229376 | tf_op jit(solution)/shard_map/concatenate | solution.py:378
  12.6 0.0 copy-done
  12.6 0.0 copy-done.1
  12.6 3.4 %collective-permute-start.2 = (bf16[224,256]{1,0:T(8,128)(2,1)S(1)}, bf16[224,256]{1,0:T(8,128)(2,1)S(1)}, u32[]{:S(2)}, u32[]{:S(2)}) collective-permute-start(bf16[224,256]{1,0:T(8,128)(2,1)S(1)} %pad_maximum_fusion), channel_id=1, source_target_pairs={{0,4},{4,8},{8,12},{12,16},{16,20},{20,24},{24,28},{1,5},{5,9},{9,... | collective-permute-start | bytes 344072 | tf_op jit(solution)/shard_map/ppermute | solution.py:374
  16.0 0.0 copy-done.4
  16.1 1.3 %collective-permute-start.3 = (bf16[224,256]{1,0:T(8,128)(2,1)S(1)}, bf16[224,256]{1,0:T(8,128)(2,1)S(1)}, u32[]{:S(2)}, u32[]{:S(2)}) collective-permute-start(bf16[224,256]{1,0:T(8,128)(2,1)S(1)} %pad_maximum_fusion.1), channel_id=1, source_target_pairs={{4,0},{8,4},{12,8},{16,12},{20,16},{24,20},{28,24},{5,1},{9,5},{13... | collective-permute-start | bytes 344072 | tf_op jit(solution)/shard_map/ppermute | solution.py:374
  17.4 1.0 %collective-permute-done.2.refs_5_ = bf16[224,256]{1,0:T(8,128)(2,1)S(1)} collective-permute-done((bf16[224,256]{1,0:T(8,128)(2,1)S(1)}, bf16[224,256]{1,0:T(8,128)(2,1)S(1)}, u32[]{:S(2)}, u32[]{:S(2)}) %collective-permute-start.2) | collective-permute-done | bytes 114720 | tf_op jit(solution)/shard_map/ppermute | solution.py:374
  18.4 0.0 copy-start.2
  18.4 4.4 %collective-permute-done.3.refs_6_ = bf16[224,256]{1,0:T(8,128)(2,1)S(1)} collective-permute-done((bf16[224,256]{1,0:T(8,128)(2,1)S(1)}, bf16[224,256]{1,0:T(8,128)(2,1)S(1)}, u32[]{:S(2)}, u32[]{:S(2)}) %collective-permute-start.3) | collective-permute-done | bytes 114720 | tf_op jit(solution)/shard_map/ppermute | solution.py:374
  22.8 0.0 copy-done.2
  22.8 0.0 copy-start.3
  22.8 0.7 copy-done.3
  23.4 27.5 %products.1 = (f32[6,160,256]{2,1,0:T(8,128)}, f32[32,128]{1,0:T(8,128)}) custom-call(bf16[6,160,256]{2,1,0:T(8,128)(2,1)} %refs_0_.1, bf16[6,160,256]{2,1,0:T(8,128)(2,1)} %refs_1_.1, s32[10,16]{1,0:T(8,128)} %refs_2_.1, bf16[160,256]{1,0:T(8,128)(2,1)} %copy-done, bf16[160,256]{1,0:T(8,128)(2,1)} %copy-done.1, bf16[224,256]{1,0:T(8,128)(2,1)} %copy-done.2, ...), custom_call_target="tpu_custom_call" | custom-call | tf_op jit(solution)/shard_map/products/pallas_call | solution.py:387
  50.9 14.4 %all_to_all.11 = f32[32,1,128]{2,1,0:T(1,128)} all-to-all(f32[32,1,128]{2,1,0:T(1,128)} %bitcast.6), channel_id=1, replica_groups=mesh['gx'=8,'gy'=4] {'gx','gy'}, dimensions={0} | all-to-all | bytes 32768 | tf_op jit(solution)/shard_map/all_to_all | solution.py:398
  65.3 2.4 %scale.1 = (f32[6,160,256]{2,1,0:T(8,128)}, f32[1,1]{1,0:T(1,128)}) custom-call(f32[6,160,256]{2,1,0:T(8,128)} %get-tuple-element.14.refs_0_, f32[32,128]{1,0:T(8,128)} %bitcast.5), custom_call_target="tpu_custom_call" | custom-call | tf_op jit(solution)/shard_map/scale/pallas_call | solution.py:403
  (3 shorter events, 0.0 us)
Async XLA Ops:
  3.8 3.7 %collective-permute-start = (bf16[160,256]{1,0:T(8,128)(2,1)}, bf16[160,256]{1,0:T(8,128)(2,1)S(1)}, u32[]{:S(2)}, u32[]{:S(2)}) collective-permute-start(bf16[160,256]{1,0:T(8,128)(2,1)} %get-tuple-element.10), channel_id=1, source_target_pairs={{0,1},{1,2},{2,3},{4,5},{5,6},{6,7},{8,9},{9,10},{10,11},{12,13},{... | collective-permute-start | bytes 245768 | tf_op jit(solution)/shard_map/ppermute | solution.py:374
  6.2 5.5 %collective-permute-start.1 = (bf16[160,256]{1,0:T(8,128)(2,1)}, bf16[160,256]{1,0:T(8,128)(2,1)S(1)}, u32[]{:S(2)}, u32[]{:S(2)}) collective-permute-start(bf16[160,256]{1,0:T(8,128)(2,1)} %get-tuple-element.11), channel_id=1, source_target_pairs={{1,0},{2,1},{3,2},{5,4},{6,5},{7,6},{9,8},{10,9},{11,10},{13,12},{... | collective-permute-start | bytes 245768 | tf_op jit(solution)/shard_map/ppermute | solution.py:374
  7.5 5.1 %copy-start = (bf16[160,256]{1,0:T(8,128)(2,1)}, bf16[160,256]{1,0:T(8,128)(2,1)S(1)}, u32[]{:S(2)}) copy-start(bf16[160,256]{1,0:T(8,128)(2,1)S(1)} %collective-permute-done.refs_3_) | copy-start | bytes 245764
  11.7 1.0 %copy-start.1 = (bf16[160,256]{1,0:T(8,128)(2,1)}, bf16[160,256]{1,0:T(8,128)(2,1)S(1)}, u32[]{:S(2)}) copy-start(bf16[160,256]{1,0:T(8,128)(2,1)S(1)} %collective-permute-done.1.refs_4_) | copy-start | bytes 245764
  11.7 4.4 %copy-start.4 = (bf16[192,256]{1,0:T(8,128)(2,1)S(1)}, bf16[192,256]{1,0:T(8,128)(2,1)}, u32[]{:S(2)}) copy-start(bf16[192,256]{1,0:T(8,128)(2,1)} %get-tuple-element.13) | copy-start | bytes 294916
  12.6 5.8 %collective-permute-start.2 = (bf16[224,256]{1,0:T(8,128)(2,1)S(1)}, bf16[224,256]{1,0:T(8,128)(2,1)S(1)}, u32[]{:S(2)}, u32[]{:S(2)}) collective-permute-start(bf16[224,256]{1,0:T(8,128)(2,1)S(1)} %pad_maximum_fusion), channel_id=1, source_target_pairs={{0,4},{4,8},{8,12},{12,16},{16,20},{20,24},{24,28},{1,5},{5,9},{9,... | collective-permute-start | bytes 344072 | tf_op jit(solution)/shard_map/ppermute | solution.py:374
  16.1 6.7 %collective-permute-start.3 = (bf16[224,256]{1,0:T(8,128)(2,1)S(1)}, bf16[224,256]{1,0:T(8,128)(2,1)S(1)}, u32[]{:S(2)}, u32[]{:S(2)}) collective-permute-start(bf16[224,256]{1,0:T(8,128)(2,1)S(1)} %pad_maximum_fusion.1), channel_id=1, source_target_pairs={{4,0},{8,4},{12,8},{16,12},{20,16},{24,20},{28,24},{5,1},{9,5},{13... | collective-permute-start | bytes 344072 | tf_op jit(solution)/shard_map/ppermute | solution.py:374
  18.4 4.4 %copy-start.2 = (bf16[224,256]{1,0:T(8,128)(2,1)}, bf16[224,256]{1,0:T(8,128)(2,1)S(1)}, u32[]{:S(2)}) copy-start(bf16[224,256]{1,0:T(8,128)(2,1)S(1)} %collective-permute-done.2.refs_5_) | copy-start | bytes 344068
  22.8 0.7 copy-start.3
where the time goes:
time: 68 us; the launch traced here: 67.7 us
  Pallas kernels  33 us (49%)
  blocking collectives  14.4 us (21%)
  waiting for transfers between devices  9.56 us (14%)
  starting transfers between devices  8.37 us (12%)
  other arithmetic  0.96 us (1%)
  between operations  0.72 us (1%)
  local copies, waits for them, and re-layouts  0.68 us (1%)
    pallas_call x1, Pallas kernels, on_device(): pl.pallas_call(main, out_shape=(jax.ShapeDtypeStruct((6, rows, cols), f32...  27.5 us
    all_to_all x1, blocking collectives, on_device(): sums = lax.all_to_all(sums, ('gx', 'gy'), 0, 0, tiled=True)  14.4 us
    ppermute x2, waiting for transfers between devices, both(): lax.ppermute(low_going, axis, down)  8.54 us
    ppermute x2, starting transfers between devices, both(): lax.ppermute(high_going, axis, up)  5.79 us
    pallas_call x1, Pallas kernels, on_device(): pl.pallas_call(pack_kernel, out_shape=(jax.ShapeDtypeStruct((rows, 2 * LA...  3.13 us
    ppermute x2, starting transfers between devices, both(): lax.ppermute(low_going, axis, down)  2.58 us
    pallas_call x1, Pallas kernels, on_device(): pl.pallas_call(scale, out_shape=(jax.ShapeDtypeStruct((6, rows, cols), f3...  2.36 us
  transfers between devices with their start and end apart: 4, of which 3 were waited for; matrix products, arithmetic and copies ran while one was open for 0% of the time, Pallas kernels for 0%

commit v1 on v0

--- a/solution.py
+++ b/solution.py
@@ -10,8 +10,6 @@
 LANES = 128
 SUB = 8
 STRIP = 16
-LOW = 13
-HIGH = 14
 PAD = 24
 epsilon = 1e-06
 f32 = jnp.float32
@@ -60,7 +58,6 @@
         return value
 
     lanes = lane_index(STRIP)
-    last = cols - LANES
     per = LANES // STRIP
 
     def block(step, carry):
@@ -70,10 +67,11 @@
             high_part = jnp.zeros((STRIP, LANES), f32)
             for index in range(group * per, min(12, (group + 1) * per)):
                 value = source(index, first)
-                place = STRIP * (index % per)
-                here = (lanes >= place) & (lanes < place + STRIP)
-                low_part = jnp.where(here, shifted(value[:, :LANES], place), low_part)
-                high_part = jnp.where(here, shifted(value[:, last:], place + STRIP), high_part)
+                ends = jnp.where(lanes < LANES // 2, value[:, :LANES], value[:, LANES:])
+                slot = index % per
+                ends = shifted(ends, STRIP * slot)
+                low_part = jnp.where(lanes // STRIP == slot, ends, low_part)
+                high_part = jnp.where(lanes // STRIP == (slot - 1) % per, ends, high_part)
             left[pl.ds(first, STRIP), group * LANES : (group + 1) * LANES] = low_part.astype(bf16)
             right[pl.ds(first, STRIP), group * LANES : (group + 1) * LANES] = high_part.astype(bf16)
         return carry
@@ -84,16 +82,17 @@
         bottom[index * STRIP : (index + 1) * STRIP, :] = source(index, rows - STRIP).astype(bf16)
 
 
-def forward(centre, plus, plus2, minus):
+def along(minus, centre, plus, plus2):
     return 27.0 * (plus - centre) - (plus2 - minus)
 
 
 def main_kernel(
-    row_parts, width, start, tensor, class_map, left, right, above, below, out, sums, field, flux, coef, mask, keep, keep2, inner
+    start, tensor, class_map, left, right, above, below, out, sums, field, flux, coef, mask, keep, keep2, inner
 ):
     rows, cols = start.shape[1:]
     tiles = field.shape[0]
     per = LANES // STRIP
+    bounds = (0, 3 * LANES // 4, cols - 3 * LANES // 4, cols)
     row_base = lax.axis_index("gx") * rows
     col_base = lax.axis_index("gy") * cols
     total_rows = rows * lax.axis_size("gx")
@@ -103,13 +102,18 @@
 
     for tile in range(tiles):
         r = lax.broadcasted_iota(jnp.int32, (deep, LANES), 0) - PAD
-        c = lax.broadcasted_iota(jnp.int32, (deep, LANES), 1) + (tile * width - LOW)
+        c = lax.broadcasted_iota(jnp.int32, (deep, LANES), 1)
+        if tile == 0:
+            c = jnp.where(c < LANES - STRIP, c, c - LANES)
+        elif tile == 1:
+            c = jnp.where(c < LANES // 2, c + LANES, c)
+        else:
+            c = jnp.where(c < STRIP, c + cols, c + LANES)
         gr, gc = r + row_base, c + col_base
         good = (gr >= 0) & (gr < total_rows) & (gc >= 0) & (gc < total_cols)
         keep[tile] = jnp.where(good, 1.0, 0.0)
         keep2[tile] = jnp.where(good, BELOW, 0.0)
-        lo = tile * width
-        mine = (r >= 0) & (r < rows) & (c >= lo) & (c < min(cols, lo + width))
+        mine = (r >= 0) & (r < rows) & (c >= bounds[tile]) & (c < bounds[tile + 1])
         inner[tile] = jnp.where(mine, 1.0, 0.0)
         edge = jnp.zeros((SUB, LANES), f32)
         for index in range(6):
@@ -119,95 +123,82 @@
 
     lanes = lane_index(STRIP)
 
-    def place(target, index, first, value, low_strip, high_strip, factor):
-        value = value * factor
-        spot = STRIP * (index % per)
-        group = index // per
-        low_part = low_strip[:, group * LANES : (group + 1) * LANES] * factor
-        high_part = high_strip[:, group * LANES : (group + 1) * LANES] * factor
+    def place(index, first, value, strips):
+        target = field if index < 6 else coef
         which = index if index < 6 else index - 6
-        for tile in range(tiles):
-            base = tile * width - LOW
-            result = jnp.zeros((STRIP, LANES), f32)
-            if base < 0:
-                result = jnp.where(lanes < -base, shifted(low_part, -(spot + STRIP + base)), result)
-            for piece in range(cols // LANES):
-                begin = piece * LANES - base
-                if begin >= LANES or begin + LANES <= 0:
-                    continue
-                here = (lanes >= begin) & (lanes < begin + LANES)
-                moved = shifted(value[:, piece * LANES : (piece + 1) * LANES], begin)
-                result = jnp.where(here, moved, result)
-            begin = cols - base
-            if begin < LANES:
-                here = (lanes >= begin) & (lanes < begin + STRIP)
-                result = jnp.where(here, shifted(high_part, begin - spot), result)
-            target[tile, which, pl.ds(first, STRIP), :] = result
+        factor = FIELD_SCALE[index] if index < 6 else TENSOR_SCALE[index - 6]
+        slot = index % per
+        ends = shifted(strips[index // per][slot % 2], -STRIP * slot)
+        one, two = value[:, :LANES], value[:, LANES:]
+        if factor != 1.0:
+            one, two, ends = one * factor, two * factor, ends * factor
+        target[0, which, pl.ds(first, STRIP), :] = jnp.where(lanes < LANES - STRIP, one, ends)
+        target[1, which, pl.ds(first, STRIP), :] = jnp.where(lanes < LANES // 2, two, one)
+        target[2, which, pl.ds(first, STRIP), :] = jnp.where(lanes < STRIP, ends, two)
+
+    def merged(low_strip, high_strip):
+        odd = (lanes // STRIP) % 2 == 1
+        pairs = []
+        for group in range(2):
+            low = low_strip[:, group * LANES : (group + 1) * LANES]
+            high = high_strip[:, group * LANES : (group + 1) * LANES]
+            pairs.append((jnp.where(odd, low, high), jnp.where(odd, high, low)))
+        return pairs
 
     def assemble(step, carry):
         first = pl.multiple_of(step * STRIP, STRIP)
-        low_strip = left[pl.ds(first, STRIP), :].astype(f32)
-        high_strip = right[pl.ds(first, STRIP), :].astype(f32)
+        strips = merged(left[pl.ds(first, STRIP), :].astype(f32), right[pl.ds(first, STRIP), :].astype(f32))
         for index in range(12):
             if index < 6:
                 value = start[index, pl.ds(first, STRIP), :].astype(f32)
-                place(field, index, PAD + first, value, low_strip, high_strip, FIELD_SCALE[index])
             else:
                 value = tensor[index - 6, pl.ds(first, STRIP), :].astype(f32)
                 if index >= 9:
                     value = value * mask[pl.ds(first, STRIP), :]
-                place(coef, index, PAD + first, value, low_strip, high_strip, TENSOR_SCALE[index - 6])
+            place(index, PAD + first, value, strips)
         return carry
 
     lax.fori_loop(0, rows // STRIP, assemble, 0)
     for strip, first in ((above, PAD - STRIP), (below, PAD + rows)):
-        low_strip = strip[12 * STRIP : 13 * STRIP, :].astype(f32)
-        high_strip = strip[13 * STRIP : 14 * STRIP, :].astype(f32)
+        strips = merged(
+            strip[12 * STRIP : 13 * STRIP, :].astype(f32), strip[13 * STRIP : 14 * STRIP, :].astype(f32)
+        )
         for index in range(12):
-            value = strip[index * STRIP : (index + 1) * STRIP, :].astype(f32)
-            factor = FIELD_SCALE[index] if index < 6 else TENSOR_SCALE[index - 6]
-            place(field if index < 6 else coef, index, first, value, low_strip, high_strip, factor)
+            place(index, first, strip[index * STRIP : (index + 1) * STRIP, :].astype(f32), strips)
 
     def load(ref, tile, index, first, offset):
         return ref[tile, index, pl.ds(first + offset, SUB), :]
 
-    def curl_forward(ref, tile, first):
+    def curl(ref, tile, first, back):
         out_parts = []
         centre = [load(ref, tile, index, first, 0) for index in range(6)]
-        for part in range(2):
-            sign = 1.0 if part == 0 else -1.0
-            x, y, z = centre[3 * part : 3 * part + 3]
-            ox, oy = centre[3 - 3 * part], centre[4 - 3 * part]
-            zi, yi = 3 * part + 2, 3 * part + 1
-            dyz = forward(z, shifted(z, -1), shifted(z, -2), shifted(z, 1))
-            dxz = forward(
-                z, load(ref, tile, zi, first, 1), load(ref, tile, zi, first, 2), load(ref, tile, zi, first, -1)
-            )
-            near = (load(ref, tile, yi, first, 1) - y) - (shifted(x, -1) - x)
-            far = (load(ref, tile, yi, first, 2) - load(ref, tile, yi, first, -1)) - (shifted(x, -2) - shifted(x, 1))
-            if part == 0:
-                out_parts.append((dyz + oy, -(ox + dxz), 27.0 * near - far))
-            else:
-                out_parts.append((dyz - oy, ox - dxz, 27.0 * near - far))
-        return out_parts
-
-    def curl_backward(ref, tile, first):
-        out_parts = []
-        centre = [load(ref, tile, index, first, 0) for index in range(6)]
+
+        def across(value):
+            if back:
+                other = shifted(value, 2)
+                return 27.0 * value + other, -shifted(27.0 * other + value, -1)
+            other = shifted(value, -2)
+            return -(27.0 * value + other), shifted(27.0 * other + value, 1)
+
+        def down(index):
+            cells = [
+                centre[index] if step == 0 else load(ref, tile, index, first, step)
+                for step in range(-1 - back, 3 - back)
+            ]
+            return along(*cells)
+
         for part in range(2):
             x, y, z = centre[3 * part : 3 * part + 3]
             ox, oy = centre[3 - 3 * part], centre[4 - 3 * part]
-            zi, yi = 3 * part + 2, 3 * part + 1
-            dyz = forward(shifted(z, 1), z, shifted(z, -1), shifted(z, 2))
-            dxz = forward(
-                load(ref, tile, zi, first, -1), z, load(ref, tile, zi, first, 1), load(ref, tile, zi, first, -2)
-            )
-            near = (y - load(ref, tile, yi, first, -1)) - (x - shifted(x, 1))
-            far = (load(ref, tile, yi, first, 1) - load(ref, tile, yi, first, -2)) - (shifted(x, -1) - shifted(x, 2))
+            xn, xf = across(x)
+            zn, zf = across(z)
+            dxz = down(3 * part + 2)
+            dxy = down(3 * part + 1)
+            hz = (dxy - xn) - xf
             if part == 0:
-                out_parts.append((dyz + oy, -(ox + dxz), 27.0 * near - far))
+                out_parts.append(((zn + oy) + zf, -(ox + dxz), hz))
             else:
-                out_parts.append((dyz - oy, ox - dxz, 27.0 * near - far))
+                out_parts.append(((zn - oy) + zf, ox - dxz, hz))
         return out_parts
 
     def contract(tile, first, parts):
@@ -223,7 +214,7 @@
             )
         return results
 
-    unroll = 4
+    unroll = 24
 
     def over(span, body, carry):
         lo = (PAD + span[0]) // SUB * SUB
@@ -254,7 +245,7 @@
 
             def first_half(first, carry):
                 m, m2 = keep[tile, pl.ds(first, SUB), :], keep2[tile, pl.ds(first, SUB), :]
-                for part, (hx, hy, hz) in enumerate(curl_forward(field, tile, first)):
+                for part, (hx, hy, hz) in enumerate(curl(field, tile, first, 0)):
                     flux[tile, 3 * part, pl.ds(first, SUB), :] = hx * m2
                     flux[tile, 3 * part + 1, pl.ds(first, SUB), :] = hy * m2
                     flux[tile, 3 * part + 2, pl.ds(first, SUB), :] = hz * m
@@ -264,7 +255,7 @@
 
             def second_half(first, carry):
                 flat, upright = carry
-                results = contract(tile, first, curl_backward(flux, tile, first))
+                results = contract(tile, first, curl(flux, tile, first, 1))
                 for part, triple in enumerate(results):
                     for axis in range(3):
                         field[tile, 3 * part + axis, pl.ds(first, SUB), :] = triple[axis]
@@ -289,8 +280,8 @@
 
         def pair(first, carry):
             flat, upright = carry
-            one = curl_forward(field, tile, first)
-            two = curl_forward(flux, tile, first)
+            one = curl(field, tile, first, 0)
+            two = curl(flux, tile, first, 0)
             own = inner[tile, pl.ds(first, SUB), :]
             flat = flat + own * (
                 (one[0][0] * two[0][0] + one[0][1] * two[0][1]) + (one[1][0] * two[1][0] + one[1][1] * two[1][1])
@@ -316,17 +307,9 @@
     def collect(step, carry):
         first = pl.multiple_of(step * SUB, SUB)
         for index in range(6):
-            for piece in range(cols // LANES):
-                result = zero
-                for tile in range(tiles):
-                    begin = tile * width - piece * LANES
-                    end = min(cols, (tile + 1) * width) - piece * LANES
-                    if end <= 0 or begin >= LANES:
-                        continue
-                    moved = shifted(field[tile, index, pl.ds(PAD + first, SUB), :], begin - LOW)
-                    here = (sub_lanes >= begin) & (sub_lanes < end)
-                    result = jnp.where(here, moved, result)
-                out[index, pl.ds(first, SUB), piece * LANES : (piece + 1) * LANES] = result
+            parts = [field[tile, index, pl.ds(PAD + first, SUB), :] for tile in range(tiles)]
+            out[index, pl.ds(first, SUB), :LANES] = jnp.where(sub_lanes < bounds[1], parts[0], parts[1])
+            out[index, pl.ds(first, SUB), LANES:] = jnp.where(sub_lanes < bounds[2] - LANES, parts[1], parts[2])
         return carry
 
     lax.fori_loop(0, rows // SUB, collect, 0)
@@ -349,8 +332,9 @@
     rows, cols = start_field.shape[1:]
     devices = lax.axis_size("gx") * lax.axis_size("gy")
     cell_count = rows * cols * devices
-    tiles = -(-cols // (LANES - LOW - HIGH))
-    width = -(-cols // tiles)
+    if cols != 2 * LANES or rows % STRIP:
+        raise ValueError("block shape")
+    tiles = 3
     whole = pl.BlockSpec(memory_space=pltpu.VMEM)
     strip_rows = 12 * STRIP
     left, right, top, bottom = pl.pallas_call(
@@ -381,11 +365,8 @@
     plane = pltpu.VMEM((tiles, deep, LANES), f32)
     stack = pltpu.VMEM((tiles, 6, deep, LANES), f32)
 
-    def main(*refs):
-        main_kernel(None, width, *refs)
-
     image, sums = pl.pallas_call(
-        main,
+        main_kernel,
         out_shape=(
             jax.ShapeDtypeStruct((6, rows, cols), f32),
             jax.ShapeDtypeStruct((devices, LANES), f32),

time: 68 us -> 52.4 us (0.77)
  Pallas kernels: 33 us -> 17.4 us
    pallas_call x1, Pallas kernels: 27.5 us -> 12 us  [on_device(): pl.pallas_call(main_kernel, out_shape=(jax.ShapeDtypeStruct((6, rows, col...]
where the time goes in v1:
time: 52.4 us; the launch traced here: 52.1 us
  Pallas kernels  17.4 us (33%)
  blocking collectives  14.4 us (27%)
  waiting for transfers between devices  9.56 us (18%)
  starting transfers between devices  8.37 us (16%)
  other arithmetic  0.96 us (2%)
  between operations  0.72 us (1%)
  local copies, waits for them, and re-layouts  0.68 us (1%)
    all_to_all x1, blocking collectives, on_device(): sums = lax.all_to_all(sums, ('gx', 'gy'), 0, 0, tiled=True)  14.4 us
    pallas_call x1, Pallas kernels, on_device(): pl.pallas_call(main_kernel, out_shape=(jax.ShapeDtypeStruct((6, rows, col...  12 us
    ppermute x2, waiting for transfers between devices, both(): lax.ppermute(low_going, axis, down)  8.54 us
    ppermute x2, starting transfers between devices, both(): lax.ppermute(high_going, axis, up)  5.79 us
    pallas_call x1, Pallas kernels, on_device(): pl.pallas_call(pack_kernel, out_shape=(jax.ShapeDtypeStruct((rows, 2 * LA...  3.04 us
    ppermute x2, starting transfers between devices, both(): lax.ppermute(low_going, axis, down)  2.58 us
    pallas_call x1, Pallas kernels, on_device(): pl.pallas_call(scale, out_shape=(jax.ShapeDtypeStruct((6, rows, cols), f3...  2.36 us
  transfers between devices with their start and end apart: 4, of which 3 were waited for; matrix products, arithmetic and copies ran while one was open for 0% of the time, Pallas kernels for 0%

profile of v1, /device:TPU:0, one launch (start us, length us, event | category | flops | bytes accessed | tf_op | source)
XLA Modules:
  0.0 52.1 jit_solution(11124370494287597979)
XLA Ops:
  0.6 3.0 %pack.1 = (bf16[160,256]{1,0:T(8,128)(2,1)}, bf16[160,256]{1,0:T(8,128)(2,1)}, bf16[192,256]{1,0:T(8,128)(2,1)}, bf16[192,256]{1,0:T(8,128)(2,1)}) custom-call(bf16[6,160,256]{2,1,0:T(8,128)(2,1)} %start.3, bf16[6,160,256]{2,1,0:T(8,128)(2,1)} %tensor.3, s32[10,16]{1,0:T(8,128)} %class_map.3), custom_call_target="tpu_custom_call" | custom-call | tf_op jit(solution)/shard_map/pack/pallas_call | solution.py:340
  3.7 2.4 %collective-permute-start = (bf16[160,256]{1,0:T(8,128)(2,1)}, bf16[160,256]{1,0:T(8,128)(2,1)S(1)}, u32[]{:S(2)}, u32[]{:S(2)}) collective-permute-start(bf16[160,256]{1,0:T(8,128)(2,1)} %get-tuple-element.10), channel_id=1, source_target_pairs={{0,1},{1,2},{2,3},{4,5},{5,6},{6,7},{8,9},{9,10},{10,11},{12,13},{... | collective-permute-start | bytes 245768 | tf_op jit(solution)/shard_map/ppermute | solution.py:358
  6.1 1.3 %collective-permute-start.1 = (bf16[160,256]{1,0:T(8,128)(2,1)}, bf16[160,256]{1,0:T(8,128)(2,1)S(1)}, u32[]{:S(2)}, u32[]{:S(2)}) collective-permute-start(bf16[160,256]{1,0:T(8,128)(2,1)} %get-tuple-element.11), channel_id=1, source_target_pairs={{1,0},{2,1},{3,2},{5,4},{6,5},{7,6},{9,8},{10,9},{11,10},{13,12},{... | collective-permute-start | bytes 245768 | tf_op jit(solution)/shard_map/ppermute | solution.py:358
  7.4 0.0 collective-permute-done.left
  7.4 0.0 copy-start
  7.4 4.2 %collective-permute-done.1.right = bf16[160,256]{1,0:T(8,128)(2,1)S(1)} collective-permute-done((bf16[160,256]{1,0:T(8,128)(2,1)}, bf16[160,256]{1,0:T(8,128)(2,1)S(1)}, u32[]{:S(2)}, u32[]{:S(2)}) %collective-permute-start.1) | collective-permute-done | bytes 81952 | tf_op jit(solution)/shard_map/ppermute | solution.py:358
  11.6 0.0 copy-start.1
  11.6 0.0 copy-start.4
  11.6 0.9 %pad_maximum_fusion = bf16[224,256]{1,0:T(8,128)(2,1)S(1)} fusion(bf16[16,256]{1,0:T(8,128)(2,1)S(1)} %get-tuple-element.21, bf16[16,256]{1,0:T(8,128)(2,1)S(1)} %get-tuple-element.19, bf16[192,256]{1,0:T(8,128)(2,1)} %get-tuple-element.12), kind=kLoop, calls=%fused_computation | loop fusion | flops 344064 | bytes 229376 | tf_op jit(solution)/shard_map/concatenate | solution.py:362
  12.5 0.0 copy-done
  12.5 0.0 copy-done.1
  12.5 3.4 %collective-permute-start.2 = (bf16[224,256]{1,0:T(8,128)(2,1)S(1)}, bf16[224,256]{1,0:T(8,128)(2,1)S(1)}, u32[]{:S(2)}, u32[]{:S(2)}) collective-permute-start(bf16[224,256]{1,0:T(8,128)(2,1)S(1)} %pad_maximum_fusion), channel_id=1, source_target_pairs={{0,4},{4,8},{8,12},{12,16},{16,20},{20,24},{24,28},{1,5},{5,9},{9,... | collective-permute-start | bytes 344072 | tf_op jit(solution)/shard_map/ppermute | solution.py:358
  15.9 0.0 copy-done.4
  16.0 1.3 %collective-permute-start.3 = (bf16[224,256]{1,0:T(8,128)(2,1)S(1)}, bf16[224,256]{1,0:T(8,128)(2,1)S(1)}, u32[]{:S(2)}, u32[]{:S(2)}) collective-permute-start(bf16[224,256]{1,0:T(8,128)(2,1)S(1)} %pad_maximum_fusion.1), channel_id=1, source_target_pairs={{4,0},{8,4},{12,8},{16,12},{20,16},{24,20},{28,24},{5,1},{9,5},{13... | collective-permute-start | bytes 344072 | tf_op jit(solution)/shard_map/ppermute | solution.py:358
  17.3 1.0 %collective-permute-done.2.above = bf16[224,256]{1,0:T(8,128)(2,1)S(1)} collective-permute-done((bf16[224,256]{1,0:T(8,128)(2,1)S(1)}, bf16[224,256]{1,0:T(8,128)(2,1)S(1)}, u32[]{:S(2)}, u32[]{:S(2)}) %collective-permute-start.2) | collective-permute-done | bytes 114720 | tf_op jit(solution)/shard_map/ppermute | solution.py:358
  18.3 0.0 copy-start.2
  18.3 4.4 %collective-permute-done.3.below = bf16[224,256]{1,0:T(8,128)(2,1)S(1)} collective-permute-done((bf16[224,256]{1,0:T(8,128)(2,1)S(1)}, bf16[224,256]{1,0:T(8,128)(2,1)S(1)}, u32[]{:S(2)}, u32[]{:S(2)}) %collective-permute-start.3) | collective-permute-done | bytes 114720 | tf_op jit(solution)/shard_map/ppermute | solution.py:358
  22.7 0.0 copy-done.2
  22.7 0.0 copy-start.3
  22.7 0.7 %copy-done.3 = bf16[224,256]{1,0:T(8,128)(2,1)} copy-done((bf16[224,256]{1,0:T(8,128)(2,1)}, bf16[224,256]{1,0:T(8,128)(2,1)S(1)}, u32[]{:S(2)}) %copy-start.3) | copy-done | bytes 114712
  23.3 12.0 %products.1 = (f32[6,160,256]{2,1,0:T(8,128)}, f32[32,128]{1,0:T(8,128)}) custom-call(bf16[6,160,256]{2,1,0:T(8,128)(2,1)} %start.3, bf16[6,160,256]{2,1,0:T(8,128)(2,1)} %tensor.3, s32[10,16]{1,0:T(8,128)} %class_map.3, bf16[160,256]{1,0:T(8,128)(2,1)} %copy-done, bf16[160,256]{1,0:T(8,128)(2,1)} %copy-done.1, bf16[224,256]{1,0:T(8,128)(2,1)} %copy-done.2, ...), custom_call_target="tpu_custom_call" | custom-call | tf_op jit(solution)/shard_map/products/pallas_call | solution.py:368
  35.3 14.4 %all_to_all.11 = f32[32,1,128]{2,1,0:T(1,128)} all-to-all(f32[32,1,128]{2,1,0:T(1,128)} %bitcast.6), channel_id=1, replica_groups=mesh['gx'=8,'gy'=4] {'gx','gy'}, dimensions={0} | all-to-all | bytes 32768 | tf_op jit(solution)/shard_map/all_to_all | solution.py:379
  49.7 2.4 %scale.1 = (f32[6,160,256]{2,1,0:T(8,128)}, f32[1,1]{1,0:T(1,128)}) custom-call(f32[6,160,256]{2,1,0:T(8,128)} %get-tuple-element.14.refs_0_, f32[32,128]{1,0:T(8,128)} %bitcast.5), custom_call_target="tpu_custom_call" | custom-call | tf_op jit(solution)/shard_map/scale/pallas_call | solution.py:384
  (3 shorter events, 0.0 us)
Async XLA Ops:
  3.7 3.7 %collective-permute-start = (bf16[160,256]{1,0:T(8,128)(2,1)}, bf16[160,256]{1,0:T(8,128)(2,1)S(1)}, u32[]{:S(2)}, u32[]{:S(2)}) collective-permute-start(bf16[160,256]{1,0:T(8,128)(2,1)} %get-tuple-element.10), channel_id=1, source_target_pairs={{0,1},{1,2},{2,3},{4,5},{5,6},{6,7},{8,9},{9,10},{10,11},{12,13},{... | collective-permute-start | bytes 245768 | tf_op jit(solution)/shard_map/ppermute | solution.py:358
  6.1 5.5 %collective-permute-start.1 = (bf16[160,256]{1,0:T(8,128)(2,1)}, bf16[160,256]{1,0:T(8,128)(2,1)S(1)}, u32[]{:S(2)}, u32[]{:S(2)}) collective-permute-start(bf16[160,256]{1,0:T(8,128)(2,1)} %get-tuple-element.11), channel_id=1, source_target_pairs={{1,0},{2,1},{3,2},{5,4},{6,5},{7,6},{9,8},{10,9},{11,10},{13,12},{... | collective-permute-start | bytes 245768 | tf_op jit(solution)/shard_map/ppermute | solution.py:358
  7.4 5.1 %copy-start = (bf16[160,256]{1,0:T(8,128)(2,1)}, bf16[160,256]{1,0:T(8,128)(2,1)S(1)}, u32[]{:S(2)}) copy-start(bf16[160,256]{1,0:T(8,128)(2,1)S(1)} %collective-permute-done.left) | copy-start | bytes 245764
  11.6 1.0 %copy-start.1 = (bf16[160,256]{1,0:T(8,128)(2,1)}, bf16[160,256]{1,0:T(8,128)(2,1)S(1)}, u32[]{:S(2)}) copy-start(bf16[160,256]{1,0:T(8,128)(2,1)S(1)} %collective-permute-done.1.right) | copy-start | bytes 245764
  11.6 4.4 %copy-start.4 = (bf16[192,256]{1,0:T(8,128)(2,1)S(1)}, bf16[192,256]{1,0:T(8,128)(2,1)}, u32[]{:S(2)}) copy-start(bf16[192,256]{1,0:T(8,128)(2,1)} %get-tuple-element.13) | copy-start | bytes 294916
  12.5 5.8 %collective-permute-start.2 = (bf16[224,256]{1,0:T(8,128)(2,1)S(1)}, bf16[224,256]{1,0:T(8,128)(2,1)S(1)}, u32[]{:S(2)}, u32[]{:S(2)}) collective-permute-start(bf16[224,256]{1,0:T(8,128)(2,1)S(1)} %pad_maximum_fusion), channel_id=1, source_target_pairs={{0,4},{4,8},{8,12},{12,16},{16,20},{20,24},{24,28},{1,5},{5,9},{9,... | collective-permute-start | bytes 344072 | tf_op jit(solution)/shard_map/ppermute | solution.py:358
  16.0 6.7 %collective-permute-start.3 = (bf16[224,256]{1,0:T(8,128)(2,1)S(1)}, bf16[224,256]{1,0:T(8,128)(2,1)S(1)}, u32[]{:S(2)}, u32[]{:S(2)}) collective-permute-start(bf16[224,256]{1,0:T(8,128)(2,1)S(1)} %pad_maximum_fusion.1), channel_id=1, source_target_pairs={{4,0},{8,4},{12,8},{16,12},{20,16},{24,20},{28,24},{5,1},{9,5},{13... | collective-permute-start | bytes 344072 | tf_op jit(solution)/shard_map/ppermute | solution.py:358
  18.3 4.4 %copy-start.2 = (bf16[224,256]{1,0:T(8,128)(2,1)}, bf16[224,256]{1,0:T(8,128)(2,1)S(1)}, u32[]{:S(2)}) copy-start(bf16[224,256]{1,0:T(8,128)(2,1)S(1)} %collective-permute-done.2.above) | copy-start | bytes 344068
  22.7 0.7 %copy-start.3 = (bf16[224,256]{1,0:T(8,128)(2,1)}, bf16[224,256]{1,0:T(8,128)(2,1)S(1)}, u32[]{:S(2)}) copy-start(bf16[224,256]{1,0:T(8,128)(2,1)S(1)} %collective-permute-done.3.below) | copy-start | bytes 344068
